TPU v7x, 128 devices: a whole 4x4x4 slice. The times are simulated.
128 devices in a mesh: edp: 2 (over y_hi), ep: 64 (over y_lo, z, x, core).
Axes of the slice: x: 4, y: 4 (y_hi: 2, y_lo: 2; y = y_hi * 2 + y_lo), z: 4, core: 2. Of those that a mesh axis runs over, the one named last changes fastest.
Arguments:
- tokens: bfloat16 [16384, 2048], P(('edp', 'ep')), may hold values from -6 to 6
- routes: int32 [16384, 8], P(('edp', 'ep')), may hold values from 0 to 63, all different within a row; in each aligned block of 128 rows (0 to 127, 128 to 255, ...) at most 24 rows name the same one
- gate_weights: float32 [16384, 8], P(('edp', 'ep')), may hold values from 0.05 to 0.5
- w_gate: bfloat16 [64, 2048, 768], P('ep'), may hold values from -0.125 to 0.125
- w_up: bfloat16 [64, 2048, 768], P('ep'), may hold values from -0.125 to 0.125
- w_down: bfloat16 [64, 768, 2048], P('ep'), may hold values from -0.21875 to 0.21875
- saved_inputs: bfloat16 [64, 512, 2048], P('ep', 'edp'), may hold values from -6 to 6
- saved_cotangent: bfloat16 [64, 512, 2048], P('ep', 'edp'), may hold values from -0.59765625 to 0.59765625
Outputs:
- mixed: bfloat16 [16384, 2048], P(('edp', 'ep'))
- grad_gate: float32 [64, 2048, 768], P('ep', 'edp')
- grad_up: float32 [64, 2048, 768], P('ep', 'edp')
- grad_down: float32 [64, 768, 2048], P('ep', 'edp')
Inputs may be any that keep to these rules, and one draw needn't show every extreme that they name: `routes`: each token names 8 different experts. In each aligned block of 128 tokens (the tokens of one device) no expert is named more than 24 times, a bound that some block reaches in every draw.
All inputs are finite; a program needn't handle non-finite values.
Results may differ from a plain program's by a relative error of at most 0.006.
Values may be sent and summed in bfloat16 or wider, within the bound.
A program may use at most 128 MiB of HBM per device.

v0:
```python
import jax
import jax.numpy as jnp
from jax import lax
from jax.experimental import pallas as pl
from jax.experimental.pallas import tpu as pltpu
from jax.sharding import PartitionSpec as P

CAP = 24
SIDE = 4
TARGETS = 8
PAIR = 2 * CAP
CHUNK = TARGETS * PAIR
TILE = 256
ORDER = (0, 1, 3, 2)
BF = jnp.bfloat16
F32 = jnp.float32


def dot(a, b, dims=((1,), (0,))):
    return lax.dot_general(a, b, (dims, ((), ())), preferred_element_type=F32)


def tile(n, size=TILE):
    return pl.ds(pl.multiple_of(n * size, size), size)


def loop(count, body):
    def step(n, carry):
        body(n)
        return carry

    lax.fori_loop(0, count, step, 0)


def kernel(
    routes, gates, tokens, w_gate, w_up, w_down, saved_x, saved_y,
    mixed, grad_gate, grad_up, grad_down,
    wg, wu, wd, blocks, aux, aux32, hot, hot_lhs, mix_lhs, packed, recv, back, part, gathered,
    y_send, y_recv, total, xs, ys, hid, dgs, dus, hbuf, stage_a, stage_b,
    load_sem, y_s, y_r, a_s, a_r, b_s, b_r, rb_s, rb_r, ra_s, ra_r, ry_s, ry_r, e_s, e_r, out_sem, mix_sem,
):
    width = blocks.shape[-1]
    rows = blocks.shape[1] // 2
    hidden_width = wg.shape[1]
    half_width = width // 2
    half_hidden = hidden_width // 2
    tiles = width // TILE

    me = lax.axis_index("ep")
    replica = lax.axis_index("edp")
    core = lax.rem(me, 2)
    x = lax.rem(me // 2, SIDE)
    z = lax.rem(me // (2 * SIDE), SIDE)
    y = me // (2 * SIDE * SIDE)
    a = z * (1 - core) + x * core
    b = x * (1 - core) + z * core

    def place(yy, aa, bb, cc):
        aa = lax.rem(aa, SIDE)
        bb = lax.rem(bb, SIDE)
        zz = aa * (1 - core) + bb * core
        xx = bb * (1 - core) + aa * core
        return ((yy * SIDE + zz) * SIDE + xx) * 2 + cc

    def at(index):
        return (replica, index)

    y_peer = at(place(1 - y, a, b, core))
    edp_peer = (1 - replica, me)

    def forward_to(t):
        f, g = t // 2, t % 2
        return place(y, a, b + f, core if g == 0 else 1 - core)

    def forwarder(t):
        f, g = t // 2, t % 2
        if g == 0:
            return place(y, a, b + SIDE - f, core)
        return place(y, a + SIDE - f, b, 1 - core)

    loads = [
        pltpu.make_async_copy(tokens, blocks.at[0, 0:rows], load_sem.at[0]),
        pltpu.make_async_copy(saved_x.at[0], xs.at[0], load_sem.at[1]),
        pltpu.make_async_copy(saved_y.at[0], ys.at[0], load_sem.at[2]),
        pltpu.make_async_copy(w_gate.at[0], wg, load_sem.at[3]),
        pltpu.make_async_copy(w_up.at[0], wu, load_sem.at[4]),
        pltpu.make_async_copy(w_down.at[0], wd, load_sem.at[5]),
    ]
    for copy in loads:
        copy.start()

    barrier = pltpu.get_barrier_semaphore()
    peers = [y_peer, edp_peer]
    peers += [at(place(y, a + d, b, core)) for d in range(1, SIDE)]
    peers += [at(place(y, a, b + d, core)) for d in range(1, SIDE)]
    peers += [at(place(y, a, b + d, 1 - core)) for d in range(SIDE)]
    peers += [at(place(y, a + d, b, 1 - core)) for d in range(1, SIDE)]
    for peer in peers:
        pl.semaphore_signal(barrier, inc=1, device_id=peer, device_id_type=pl.DeviceIdType.MESH)

    experts = TARGETS * TARGETS
    names = lax.broadcasted_iota(jnp.int32, (experts, rows), 0)
    named = jnp.zeros((experts, rows), F32)
    weight = jnp.zeros((experts, rows), F32)
    for k in range(routes.shape[0]):
        match = names == routes[k : k + 1, :]
        named = named + jnp.where(match, 1.0, 0.0)
        weight = weight + jnp.where(match, gates[k : k + 1, :], 0.0)
    earlier = (
        lax.broadcasted_iota(jnp.int32, (rows, rows), 0)
        < lax.broadcasted_iota(jnp.int32, (rows, rows), 1)
    )
    earlier = jnp.where(earlier, 1.0, 0.0).astype(BF)
    count = dot(named.astype(BF), earlier)
    aux[0, 0, 0:experts, :] = jnp.where(named > 0.5, count, -1.0).astype(BF)
    aux[0, 0, experts : 2 * experts, :] = weight.astype(BF)
    hot[...] = jnp.zeros_like(hot)

    pl.semaphore_wait(barrier, len(peers))
    loads[0].wait()

    def remote(src, dst, send, receive, peer):
        return pltpu.make_async_remote_copy(
            src_ref=src, dst_ref=dst, send_sem=send, recv_sem=receive,
            device_id=peer, device_id_type=pl.DeviceIdType.MESH,
        )

    own, other = pl.ds(0, rows), pl.ds(rows, rows)
    y_copies = [
        remote(aux.at[0, 0], aux.at[0, 1], y_s.at[0], y_r.at[0], y_peer),
        remote(blocks.at[0, own], blocks.at[0, other], y_s.at[1], y_r.at[1], y_peer),
    ]
    for copy in y_copies:
        copy.start()
    a_copies = {}
    for d in (1, 3, 2):
        peer = at(place(y, a + d, b, core))
        for dy, where in ((0, own), (1, other)):
            a_copies[d, dy] = [
                remote(aux.at[0, dy], aux.at[d, dy], a_s.at[d - 1, 2 * dy], a_r.at[d - 1, 2 * dy], peer),
                remote(blocks.at[0, where], blocks.at[d, where], a_s.at[d - 1, 2 * dy + 1],
                       a_r.at[d - 1, 2 * dy + 1], peer),
            ]
    for d in (1, 3, 2):
        for copy in a_copies[d, 0]:
            copy.start()
    loads[1].wait()
    loads[2].wait()
    e_copies = [
        remote(xs.at[0], xs.at[1], e_s.at[0], e_r.at[0], edp_peer),
        remote(ys.at[0], ys.at[1], e_s.at[1], e_r.at[1], edp_peer),
    ]
    for copy in e_copies:
        copy.start()

    def backward(r):
        def body(n):
            cols = tile(n)
            g = dot(xs[r], wg[:, cols])
            u = dot(xs[r], wu[:, cols])
            dh = dot(ys[r], wd[cols, :], ((1,), (1,)))
            s = jax.nn.sigmoid(g)
            act = g * s
            hid[r, :, cols] = (act * u).astype(BF)
            dgs[r, :, cols] = (dh * u * s * (1.0 + g * (1.0 - s))).astype(BF)
            dus[r, :, cols] = (dh * act).astype(BF)

        loop(hidden_width // TILE, body)

    def fill_hot(d, weighted):
        slots = lax.broadcasted_iota(jnp.int32, (CAP, rows), 0).astype(F32)
        for dy in range(2):
            aux32[dy] = aux[d, dy].astype(F32)
        for t in range(TARGETS):
            e = forward_to(t)
            for dy in range(2):
                hit = aux32[dy, pl.ds(e, 1), :] == slots
                value = aux32[dy, pl.ds(e + experts, 1), :] if weighted else 1.0
                at_row = PAIR * t + CAP * dy
                hot[at_row : at_row + CAP, rows * dy : rows * dy + rows] = jnp.where(hit, value, 0.0)

    def b_copy(d, t):
        span = pl.ds(PAIR * t, PAIR)
        return remote(packed.at[d, span], recv.at[d, span], b_s.at[d, t], b_r.at[d, t], at(forward_to(t)))

    def rb_copy(d, t):
        span = pl.ds(PAIR * t, PAIR)
        return remote(recv.at[d, span], back.at[d, span], rb_s.at[d, t], rb_r.at[d, t], at(forwarder(t)))

    def pack(d):
        fill_hot(d, False)
        hot_lhs[...] = hot[...].astype(BF)

        def body(n):
            cols = tile(n)
            rows_out = dot(hot_lhs[...], blocks[d, :, cols]).astype(BF)
            packed[d, :, cols] = rows_out
            recv[d, 0:PAIR, cols] = rows_out[0:PAIR]

        loop(tiles, body)
        for t in range(1, TARGETS):
            b_copy(d, t).start()

    def mlp(d):
        for t in range(1, TARGETS):
            b_copy(d, t).wait_recv()

        def up(n):
            cols = tile(n)
            g = dot(recv[d], wg[:, cols])
            u = dot(recv[d], wu[:, cols])
            hbuf[:, cols] = (g * jax.nn.sigmoid(g) * u).astype(BF)

        loop(hidden_width // TILE, up)

        def down(n):
            cols = tile(n)
            out = dot(hbuf[...], wd[:, cols]).astype(BF)
            recv[d, :, cols] = out
            back[d, 0:PAIR, cols] = out[0:PAIR]

        loop(tiles, down)
        for t in range(1, TARGETS):
            rb_copy(d, t).start()

    def ra_copy(d, dy):
        span = pl.ds(rows * dy, rows)
        return remote(part.at[d, span], gathered.at[d - 1, span], ra_s.at[d - 1, dy], ra_r.at[d - 1, dy],
                      at(place(y, a + SIDE - d, b, core)))

    def combine(d):
        fill_hot(d, True)
        mix_lhs[...] = hot[...].T.astype(BF)
        for t in range(1, TARGETS):
            rb_copy(d, t).wait_recv()

        def body(n):
            cols = tile(n)
            part[d, :, cols] = dot(mix_lhs[...], back[d, :, cols]).astype(BF)

        loop(tiles, body)
        if d > 0:
            for dy in (1, 0):
                ra_copy(d, dy).start()

    def out_copies(kind, n):
        slot = lax.rem(n, 2)
        if kind == 2:
            return pltpu.make_async_copy(stage_b.at[slot], grad_down.at[0, :, tile(n, stage_b.shape[2])],
                                         out_sem.at[2, slot])
        ref = grad_gate if kind == 0 else grad_up
        return pltpu.make_async_copy(stage_a.at[kind, slot], ref.at[0, tile(n)], out_sem.at[kind, slot])

    def weight_grads():
        def body(n):
            @pl.when(n >= 2)
            def _():
                for kind in range(2):
                    out_copies(kind, n - 2).wait()

            cols = pl.ds(pl.multiple_of(replica * half_width + n * TILE, TILE), TILE)
            slot = lax.rem(n, 2)
            for kind, source in ((0, dgs), (1, dus)):
                sums = [dot(xs[r, :, cols], source[r], ((0,), (0,))).astype(BF).astype(F32) for r in range(2)]
                stage_a[kind, slot] = sums[0] + sums[1]
                out_copies(kind, n).start()

        count = half_width // TILE
        loop(count, body)
        size = stage_b.shape[2]

        def down(n):
            @pl.when(n >= 2)
            def _():
                out_copies(2, n - 2).wait()

            own_cols = pl.ds(pl.multiple_of(replica * half_hidden, 128), half_hidden)
            slot = lax.rem(n, 2)
            sums = [
                dot(hid[r, :, own_cols], ys[r, :, tile(n, size)], ((0,), (0,))).astype(BF).astype(F32)
                for r in range(2)
            ]
            stage_b[slot] = sums[0] + sums[1]
            out_copies(2, n).start()

        loop(width // size, down)
        for n in (count - 2, count - 1):
            for kind in range(2):
                out_copies(kind, n).wait()
        for n in (width // size - 2, width // size - 1):
            out_copies(2, n).wait()

    for copy in loads[3:]:
        copy.wait()
    backward(0)
    for copy in y_copies:
        copy.wait_recv()
    for d in (1, 3, 2):
        for copy in a_copies[d, 1]:
            copy.start()
    pack(0)
    for d in (1, 3):
        for dy in range(2):
            for copy in a_copies[d, dy]:
                copy.wait_recv()
        pack(d)
    mlp(0)
    for dy in range(2):
        for copy in a_copies[2, dy]:
            copy.wait_recv()
    pack(2)
    mlp(1)
    mlp(3)
    mlp(2)
    for copy in e_copies:
        copy.wait_recv()
    backward(1)
    combine(0)
    combine(1)
    combine(3)
    weight_grads()
    combine(2)
    for d in range(1, SIDE):
        ra_copy(d, 1).wait_recv()

    def sums(dy):
        span = pl.ds(rows * dy, rows)

        def body(n):
            cols = tile(n)
            value = part[0, span, cols].astype(F32)
            for d in range(1, SIDE):
                value = value + gathered[d - 1, span, cols].astype(F32)
            if dy == 1:
                y_send[:, cols] = value.astype(BF)
            else:
                total[:, cols] = value

        loop(tiles, body)

    sums(1)
    ry = remote(y_send, y_recv, ry_s, ry_r, y_peer)
    ry.start()
    for d in range(1, SIDE):
        ra_copy(d, 0).wait_recv()
    sums(0)
    ry.wait_recv()

    def finish(n):
        cols = tile(n)
        total[:, cols] = total[:, cols] + y_recv[:, cols].astype(F32)
        part[0, 0:rows, cols] = total[:, cols].astype(BF)

    loop(tiles, finish)
    last = pltpu.make_async_copy(part.at[0, 0:rows], mixed, mix_sem)
    last.start()

    for copy in y_copies + e_copies + [ry]:
        copy.wait_send()
    for d in range(1, SIDE):
        for dy in range(2):
            for copy in a_copies[d, dy]:
                copy.wait_send()
            ra_copy(d, dy).wait_send()
    for d in range(SIDE):
        for t in range(1, TARGETS):
            b_copy(d, t).wait_send()
            rb_copy(d, t).wait_send()
    last.wait()


def shards(tokens, routes, gate_weights, w_gate, w_up, w_down, saved_inputs, saved_cotangent):
    rows, width = tokens.shape
    hidden = w_gate.shape[2]
    back_rows = saved_inputs.shape[1]
    anywhere = pl.BlockSpec(memory_space=pl.ANY)
    whole = pl.BlockSpec(memory_space=pltpu.VMEM)
    dma = pltpu.SemaphoreType.DMA
    vm = pltpu.VMEM
    return pl.pallas_call(
        kernel,
        out_shape=(
            jax.ShapeDtypeStruct((rows, width), BF),
            jax.ShapeDtypeStruct((1, width // 2, hidden), F32),
            jax.ShapeDtypeStruct((1, width // 2, hidden), F32),
            jax.ShapeDtypeStruct((1, hidden // 2, width), F32),
        ),
        in_specs=[whole, whole] + [anywhere] * 6,
        out_specs=(anywhere,) * 4,
        scratch_shapes=[
            vm((width, hidden), BF), vm((width, hidden), BF), vm((hidden, width), BF),
            vm((SIDE, 2 * rows, width), BF),
            vm((SIDE, 2, 128, rows), BF), vm((2, 128, rows), F32),
            vm((CHUNK, 2 * rows), F32), vm((CHUNK, 2 * rows), BF), vm((2 * rows, CHUNK), BF),
            vm((SIDE, CHUNK, width), BF), vm((SIDE, CHUNK, width), BF), vm((SIDE, CHUNK, width), BF),
            vm((SIDE, 2 * rows, width), BF), vm((SIDE - 1, 2 * rows, width), BF),
            vm((rows, width), BF), vm((rows, width), BF), vm((rows, width), F32),
            vm((2, back_rows, width), BF), vm((2, back_rows, width), BF),
            vm((2, back_rows, hidden), BF), vm((2, back_rows, hidden), BF), vm((2, back_rows, hidden), BF),
            vm((CHUNK, hidden), BF),
            vm((2, 2, TILE, hidden), F32), vm((2, hidden // 2, 512), F32),
            dma((6,)), dma((2,)), dma((2,)), dma((3, 4)), dma((3, 4)),
            dma((SIDE, TARGETS)), dma((SIDE, TARGETS)), dma((SIDE, TARGETS)), dma((SIDE, TARGETS)),
            dma((3, 2)), dma((3, 2)), dma(()), dma(()), dma((2,)), dma((2,)), dma((3, 2)), dma(()),
        ],
        compiler_params=pltpu.CompilerParams(
            collective_id=0, has_side_effects=True, vmem_limit_bytes=62 * 1024 * 1024
        ),
        cost_estimate=pl.CostEstimate(flops=22 * 10**9, bytes_accessed=40 * 10**6, transcendentals=2 * 10**6),
    )(routes.T, gate_weights.T, tokens, w_gate, w_up, w_down, saved_inputs, saved_cotangent)


def solution(mesh):
    return jax.shard_map(
        shards,
        mesh=mesh,
        in_specs=(
            P(("edp", "ep"), None),
            P(("edp", "ep"), None),
            P(("edp", "ep"), None),
            P("ep", None, None),
            P("ep", None, None),
            P("ep", None, None),
            P("ep", "edp", None),
            P("ep", "edp", None),
        ),
        out_specs=(
            P(("edp", "ep"), None),
            P("ep", "edp", None),
            P("ep", "edp", None),
            P("ep", "edp", None),
        ),
        check_vma=False,
    )
```

profile of v0, /device:TPU:1, one launch (start us, length us, event | category | flops | bytes accessed | tf_op | source)
XLA Modules:
  0.0 149.7 jit_solution(10360733030850345935)
XLA Ops:
  0.6 138.6 %shard_map.111 = (bf16[128,2048]{1,0:T(8,128)(2,1)}, f32[1,1024,768]{2,1,0:T(8,128)}, f32[1,1024,768]{2,1,0:T(8,128)}, f32[1,384,2048]{2,1,0:T(8,128)}) custom-call(s32[8,128]{1,0:T(8,128)} %bitcast.2, f32[8,128]{1,0:T(8,128)} %bitcast.3, bf16[128,2048]{1,0:T(8,128)(2,1)} %tokens.1, bf16[1,2048,768]{2,1,0:T(8,128)(2,1)} %w_gate.1, ...), custom_call_target="tpu_custom_call" | custom-call | flops 22000001024 | bytes 40000000 | tf_op jit(solution)/shard_map/pallas_call | solution.py:380
  139.2 1.9 %copy.16 = bf16[128,2048]{1,0:T(8,128)(2,1)} copy(bf16[128,2048]{1,0:T(8,128)(2,1)} %get-tuple-element.8) | data formatting | bytes 1048576
  141.1 0.0 copy-start.1
  141.1 3.9 %copy.17 = f32[1,1024,768]{2,1,0:T(8,128)} copy(f32[1,1024,768]{2,1,0:T(8,128)} %get-tuple-element.9) | data formatting | bytes 6291456
  145.0 0.0 copy-done.1
  145.0 0.0 copy-start
  145.0 1.7 %copy.18 = f32[1,1024,768]{2,1,0:T(8,128)} copy(f32[1,1024,768]{2,1,0:T(8,128)S(1)} %copy-done.1) | data formatting | bytes 6291456
  146.7 1.4 copy-done
  148.0 1.7 %copy.19 = f32[1,384,2048]{2,1,0:T(8,128)} copy(f32[1,384,2048]{2,1,0:T(8,128)S(1)} %copy-done) | data formatting | bytes 6291456
Async XLA Ops:
  141.1 3.9 %copy-start.1 = (f32[1,1024,768]{2,1,0:T(8,128)S(1)}, f32[1,1024,768]{2,1,0:T(8,128)}, u32[]{:S(2)}) copy-start(f32[1,1024,768]{2,1,0:T(8,128)} %get-tuple-element.10) | copy-start | bytes 9437188
  145.0 3.0 %copy-start = (f32[1,384,2048]{2,1,0:T(8,128)S(1)}, f32[1,384,2048]{2,1,0:T(8,128)}, u32[]{:S(2)}) copy-start(f32[1,384,2048]{2,1,0:T(8,128)} %get-tuple-element.11) | copy-start | bytes 9437188
where the time goes:
time: 150 us
  Pallas kernels  139 us (93%)
  local copies, waits for them, and re-layouts  10.5 us (7%)
    pallas_call x1, Pallas kernels, shards(): pl.pallas_call(kernel, out_shape=(jax.ShapeDtypeStruct((rows, width), BF)...  139 us
    unnamed x8, local copies, waits for them, and re-layouts  10.5 us

commit v1 on v0

v1 whole, which is shorter than its diff:
```python
import jax
import jax.numpy as jnp
from jax import lax
from jax.experimental import pallas as pl
from jax.experimental.pallas import tpu as pltpu
from jax.sharding import PartitionSpec as P

CAP = 24
SIDE = 4
TARGETS = 8
PAIR = 2 * CAP
CHUNK = TARGETS * PAIR
TILE = 256
GROUPS = 2
COLS = 2
SEAT = {(0, 0): (0, 0), (1, 0): (0, 1), (3, 0): (1, 0), (2, 0): (1, 1),
        (0, 1): (2, 0), (3, 1): (2, 1), (1, 1): (3, 0), (2, 1): (3, 1)}
BF = jnp.bfloat16
F32 = jnp.float32


def dot(a, b, dims=((1,), (0,))):
    return lax.dot_general(a, b, (dims, ((), ())), preferred_element_type=F32)


def tile(n, size=TILE):
    return pl.ds(pl.multiple_of(n * size, size), size)


def loop(count, body):
    def step(n, carry):
        body(n)
        return carry

    lax.fori_loop(0, count, step, 0)


def kernel(
    routes, gates, tokens, w_gate, w_up, w_down, saved_x, saved_y,
    mixed, grad_gate, grad_up, grad_down,
    wg, wu, wd, blocks, aux, aux32, hot, hot_lhs, mix_lhs, packed, recv, back, part, gathered, passed,
    y_send, y_recv, total, result, xs, ys, hid, dgs, dus, hbuf, stage_a, stage_b,
    load_sem, y_s, y_r, a_s, a_r, b_s, b_r, rb_s, rb_r, rp_s, rp_r, ra_s, ra_r, ry_s, ry_r, e_s, e_r, out_sem, mix_sem,
):
    width = blocks.shape[-1]
    rows = blocks.shape[1] // 2
    hidden_width = wg.shape[1]
    half_width = width // 2
    half_hidden = hidden_width // 2
    tiles = width // TILE
    per_group = tiles // GROUPS

    me = lax.axis_index("ep")
    replica = lax.axis_index("edp")
    core = lax.rem(me, 2)
    x = lax.rem(me // 2, SIDE)
    z = lax.rem(me // (2 * SIDE), SIDE)
    y = me // (2 * SIDE * SIDE)
    a = z * (1 - core) + x * core
    b = x * (1 - core) + z * core

    def place(yy, aa, bb, cc):
        aa = lax.rem(aa, SIDE)
        bb = lax.rem(bb, SIDE)
        zz = aa * (1 - core) + bb * core
        xx = bb * (1 - core) + aa * core
        return ((yy * SIDE + zz) * SIDE + xx) * 2 + cc

    def at(index):
        return (replica, index)

    y_peer = at(place(1 - y, a, b, core))
    edp_peer = (1 - replica, me)
    ahead = at(place(y, a + 1, b, core))
    behind = at(place(y, a + SIDE - 1, b, core))

    def forward_to(t):
        f, g = t // 2, t % 2
        return place(y, a, b + f, core if g == 0 else 1 - core)

    def forwarder(t):
        f, g = t // 2, t % 2
        if g == 0:
            return place(y, a, b + SIDE - f, core)
        return place(y, a + SIDE - f, b, 1 - core)

    loads = [
        pltpu.make_async_copy(tokens, blocks.at[0, 0:rows], load_sem.at[0]),
        pltpu.make_async_copy(saved_x.at[0], xs.at[0], load_sem.at[1]),
        pltpu.make_async_copy(saved_y.at[0], ys.at[0], load_sem.at[2]),
        pltpu.make_async_copy(w_gate.at[0], wg, load_sem.at[3]),
        pltpu.make_async_copy(w_up.at[0], wu, load_sem.at[4]),
        pltpu.make_async_copy(w_down.at[0], wd, load_sem.at[5]),
    ]
    for copy in loads:
        copy.start()

    barrier = pltpu.get_barrier_semaphore()
    peers = [y_peer, edp_peer, ahead, behind]
    peers += [at(place(y, a, b + d, core)) for d in range(1, SIDE)]
    peers += [at(place(y, a, b + d, 1 - core)) for d in range(SIDE)]
    peers += [at(place(y, a + d, b, 1 - core)) for d in range(1, SIDE)]
    for peer in peers:
        pl.semaphore_signal(barrier, inc=1, device_id=peer, device_id_type=pl.DeviceIdType.MESH)

    experts = TARGETS * TARGETS
    names = lax.broadcasted_iota(jnp.int32, (experts, rows), 0)
    named = jnp.zeros((experts, rows), F32)
    weight = jnp.zeros((experts, rows), F32)
    for k in range(routes.shape[0]):
        match = names == routes[k : k + 1, :]
        named = named + jnp.where(match, 1.0, 0.0)
        weight = weight + jnp.where(match, gates[k : k + 1, :], 0.0)
    earlier = (
        lax.broadcasted_iota(jnp.int32, (rows, rows), 0)
        < lax.broadcasted_iota(jnp.int32, (rows, rows), 1)
    )
    earlier = jnp.where(earlier, 1.0, 0.0).astype(BF)
    count = dot(named.astype(BF), earlier)
    aux[0, 0, 0:experts, :] = jnp.where(named > 0.5, count, -1.0).astype(BF)
    aux[0, 0, experts : 2 * experts, :] = weight.astype(BF)
    hot[...] = jnp.zeros_like(hot)

    with jax.named_scope("barrier"):
        pl.semaphore_wait(barrier, len(peers))
        loads[0].wait()

    def remote(src, dst, send, receive, peer):
        return pltpu.make_async_remote_copy(
            src_ref=src, dst_ref=dst, send_sem=send, recv_sem=receive,
            device_id=peer, device_id_type=pl.DeviceIdType.MESH,
        )

    def half(dy):
        return pl.ds(rows * dy, rows)

    def columns(c):
        return pl.ds(c * (width // COLS), width // COLS)

    def token_copies(source, target, peer, send, receive, c):
        k, i = source
        m, j = target
        copies = [remote(blocks.at[k, half(i), columns(c)], blocks.at[m, half(j), columns(c)],
                         send.at[c], receive.at[c], peer)]
        if c == 0:
            copies.append(remote(aux.at[k, i], aux.at[m, j], send.at[COLS], receive.at[COLS], peer))
        return copies

    def y_copy(c):
        return token_copies(SEAT[0, 0], SEAT[0, 1], y_peer, y_s, y_r, c)

    def a_copy(slot, dy, c):
        source, peer = SEAT[0, dy], ahead if slot == 1 else behind
        if slot == 2 and dy == 0:
            source, peer = (SEAT[1, 0], ahead) if c == 0 else (SEAT[3, 0], behind)
        elif slot == 2:
            source, peer = SEAT[2, 0], y_peer
        return token_copies(source, SEAT[slot, dy], peer, a_s.at[2 * slot - 2 + dy],
                            a_r.at[2 * slot - 2 + dy], c)

    def begin(copies):
        for copy in copies:
            copy.start()

    def arrived(copies, name):
        with jax.named_scope(name):
            for copy in copies:
                copy.wait_recv()

    def a_start(slot, dy, c):
        begin(a_copy(slot, dy, c))

    def a_wait(slot, dy, c):
        arrived(a_copy(slot, dy, c), f"await{slot}{dy}{c}")

    e_copies = [
        remote(xs.at[0], xs.at[1], e_s.at[0], e_r.at[0], edp_peer),
        remote(ys.at[0], ys.at[1], e_s.at[1], e_r.at[1], edp_peer),
    ]

    def backward(r):
        def body(n):
            cols = tile(n)
            g = dot(xs[r], wg[:, cols])
            u = dot(xs[r], wu[:, cols])
            dh = dot(ys[r], wd[cols, :], ((1,), (1,)))
            s = jax.nn.sigmoid(g)
            act = g * s
            hid[r, :, cols] = (act * u).astype(BF)
            dgs[r, :, cols] = (dh * u * s * (1.0 + g * (1.0 - s))).astype(BF)
            dus[r, :, cols] = (dh * act).astype(BF)

        with jax.named_scope(f"bwd{r}"):
            loop(hidden_width // TILE, body)

    def fill_hot(d, weighted):
        slots = lax.broadcasted_iota(jnp.int32, (CAP, rows), 0).astype(F32)
        for dy in range(2):
            aux32[dy] = aux[d, dy].astype(F32)
        for t in range(TARGETS):
            e = forward_to(t)
            for dy in range(2):
                hit = aux32[dy, pl.ds(e, 1), :] == slots
                value = aux32[dy, pl.ds(e + experts, 1), :] if weighted else 1.0
                at_row = PAIR * t + CAP * dy
                hot[at_row : at_row + CAP, rows * dy : rows * dy + rows] = jnp.where(hit, value, 0.0)

    def b_copy(d, t):
        span = pl.ds(PAIR * t, PAIR)
        return remote(packed.at[d, span], recv.at[d, span], b_s.at[d, t], b_r.at[d, t], at(forward_to(t)))

    def group(q):
        return pl.ds(q * per_group * TILE, per_group * TILE)

    def rb_copy(d, t, q):
        span = pl.ds(PAIR * t, PAIR)
        return remote(recv.at[d, span, group(q)], back.at[d, span, group(q)], rb_s.at[q * SIDE + d, t],
                      rb_r.at[q * SIDE + d, t], at(forwarder(t)))

    def pack(d):
        with jax.named_scope(f"pack{d}"):
            fill_hot(d, False)
            hot_lhs[...] = hot[...].astype(BF)

            def body(n):
                cols = tile(n)
                rows_out = dot(hot_lhs[...], blocks[d, :, cols]).astype(BF)
                packed[d, :, cols] = rows_out
                recv[d, 0:PAIR, cols] = rows_out[0:PAIR]

            loop(tiles, body)
            for t in (4, 5, 2, 3, 6, 7, 1):
                b_copy(d, t).start()

    def up(d):
        with jax.named_scope(f"upwait{d}"):
            for t in range(1, TARGETS):
                b_copy(d, t).wait_recv()

        def body(n):
            cols = tile(n)
            g = dot(recv[d], wg[:, cols])
            u = dot(recv[d], wu[:, cols])
            hbuf[d, :, cols] = (g * jax.nn.sigmoid(g) * u).astype(BF)

        with jax.named_scope(f"up{d}"):
            loop(hidden_width // TILE, body)

    def down(d, q):
        def body(n):
            cols = tile(n + q * per_group)
            out = dot(hbuf[d], wd[:, cols]).astype(BF)
            recv[d, :, cols] = out
            back[d, 0:PAIR, cols] = out[0:PAIR]

        with jax.named_scope(f"down{d}{q}"):
            loop(per_group, body)
            for t in (4, 5, 2, 3, 6, 7, 1):
                rb_copy(d, t, q).start()

    def mix(d):
        with jax.named_scope(f"mix{d}"):
            fill_hot(d, True)
            mix_lhs[d] = hot[...].T.astype(BF)

    def ra_copy(k, q):
        i = 1 if k in (0, 2) else 0
        dy = k // 2
        side = 0 if k in (0, 3) else 1
        return remote(part.at[k, half(i), group(q)], gathered.at[2 * dy + side, :, group(q)],
                      ra_s.at[k, q], ra_r.at[2 * dy + side, q], behind if side == 0 else ahead)

    def ra_wait(k, q):
        ra_copy(k, q).wait_recv()

    def rp_copy(k, q):
        peer = y_peer if k == 3 else (behind if q == 0 else ahead)
        return remote(part.at[k, half(1), group(q)], passed.at[k // 2, :, group(q)],
                      rp_s.at[k // 2, q], rp_r.at[k // 2, q], peer)

    def ry_copy(q):
        return remote(y_send.at[:, group(q)], y_recv.at[:, group(q)], ry_s.at[q], ry_r.at[q], y_peer)

    def returned(k, q):
        with jax.named_scope(f"rbwait{k}{q}"):
            for t in range(1, TARGETS):
                rb_copy(k, t, q).wait_recv()

    def each_tile(q, body):
        loop(per_group, lambda n: body(tile(n + q * per_group)))

    def third(q):
        returned(3, q)

        def body(cols):
            part[3, :, cols] = dot(mix_lhs[3], back[3, :, cols]).astype(BF)

        with jax.named_scope(f"third{q}"):
            each_tile(q, body)
            rp_copy(3, q).start()
            ra_copy(3, q).start()

    def second(q):
        returned(2, q)

        def body(cols):
            value = dot(mix_lhs[2], back[2, :, cols])
            part[2, half(1), cols] = value[rows : 2 * rows].astype(BF)
            total[:, cols] = value[0:rows]

        with jax.named_scope(f"second{q}"):
            each_tile(q, body)
            ra_copy(2, q).start()

    def first(q):
        returned(1, q)
        arrived([rp_copy(3, q)], f"rpwait3{q}")

        def body(cols):
            value = dot(mix_lhs[1], back[1, :, cols])
            part[1, half(1), cols] = (value[rows : 2 * rows] + passed[1, :, cols].astype(F32)).astype(BF)
            if q == 0:
                part[1, half(0), cols] = value[0:rows].astype(BF)

        with jax.named_scope(f"first{q}"):
            each_tile(q, body)
            rp_copy(1, q).start()
            if q == 0:
                ra_copy(1, q).start()

    def first_late():
        q = 1
        arrived([rp_copy(1, q)], f"rpwait1{q}")

        def body(cols):
            value = dot(mix_lhs[1, half(0), :], back[1, :, cols])
            part[1, half(0), cols] = (value + passed[0, :, cols].astype(F32)).astype(BF)

        with jax.named_scope("firstlate"):
            each_tile(q, body)
            ra_copy(1, q).start()

    def zeroth(q):
        returned(0, q)
        if q == 0:
            arrived([rp_copy(1, q)], f"rpwait1{q}")

        def body(cols):
            value = dot(mix_lhs[0], back[0, :, cols])
            rest = value[rows : 2 * rows]
            if q == 0:
                rest = rest + passed[0, :, cols].astype(F32)
            part[0, half(1), cols] = rest.astype(BF)
            total[:, cols] = value[0:rows]

        with jax.named_scope(f"zeroth{q}"):
            each_tile(q, body)
            ra_copy(0, q).start()

    def home(q):
        arrived([ra_copy(3, q), ra_copy(2, q)], f"rawait{q}")

        def body(cols):
            value = total[:, cols] + gathered[2, :, cols].astype(F32) + gathered[3, :, cols].astype(F32)
            y_send[:, cols] = value.astype(BF)

        with jax.named_scope(f"home{q}"):
            each_tile(q, body)
            ry_copy(q).start()

    def mixed_copy(q):
        return pltpu.make_async_copy(result.at[:, group(q)], mixed.at[:, group(q)], mix_sem.at[q])

    def finish(q):
        arrived([ry_copy(q), ra_copy(1, q), ra_copy(0, q)], f"lastwait{q}")

        def body(cols):
            value = total[:, cols] + y_recv[:, cols].astype(F32)
            value = value + gathered[0, :, cols].astype(F32) + gathered[1, :, cols].astype(F32)
            result[:, cols] = value.astype(BF)

        each_tile(q, body)
        mixed_copy(q).start()

    def out_copies(kind, n):
        slot = lax.rem(n, 2)
        if kind == 2:
            return pltpu.make_async_copy(stage_b.at[slot], grad_down.at[0, :, tile(n, stage_b.shape[2])],
                                         out_sem.at[2, slot])
        ref = grad_gate if kind == 0 else grad_up
        return pltpu.make_async_copy(stage_a.at[kind, slot], ref.at[0, tile(n)], out_sem.at[kind, slot])

    def in_weight_grads():
        def body(n):
            @pl.when(n >= 2)
            def _():
                for kind in range(2):
                    out_copies(kind, n - 2).wait()

            cols = pl.ds(pl.multiple_of(replica * half_width + n * TILE, TILE), TILE)
            slot = lax.rem(n, 2)
            for kind, source in ((0, dgs), (1, dus)):
                sums = [dot(xs[r, :, cols], source[r], ((0,), (0,))).astype(BF).astype(F32) for r in range(2)]
                stage_a[kind, slot] = sums[0] + sums[1]
                out_copies(kind, n).start()

        count = half_width // TILE
        with jax.named_scope("gradin"):
            loop(count, body)
            for n in (count - 2, count - 1):
                for kind in range(2):
                    out_copies(kind, n).wait()

    def down_weight_grad():
        size = stage_b.shape[2]

        def body(n):
            @pl.when(n >= 2)
            def _():
                out_copies(2, n - 2).wait()

            own_cols = pl.ds(pl.multiple_of(replica * half_hidden, 128), half_hidden)
            slot = lax.rem(n, 2)
            sums = [
                dot(hid[r, :, own_cols], ys[r, :, tile(n, size)], ((0,), (0,))).astype(BF).astype(F32)
                for r in range(2)
            ]
            stage_b[slot] = sums[0] + sums[1]
            out_copies(2, n).start()

        with jax.named_scope("graddown"):
            loop(width // size, body)
            for n in (width // size - 2, width // size - 1):
                out_copies(2, n).wait()

    begin(y_copy(0))
    a_start(1, 0, 0)
    a_start(3, 0, 1)
    a_start(1, 0, 1)
    a_start(3, 0, 0)
    begin(y_copy(1))
    with jax.named_scope("wload"):
        for copy in loads[1:]:
            copy.wait()
    backward(0)
    a_wait(1, 0, 0)
    a_start(2, 0, 0)
    a_wait(3, 0, 1)
    a_start(2, 0, 1)
    arrived(y_copy(0), "ywait0")
    a_start(1, 1, 0)
    a_start(3, 1, 0)
    a_wait(1, 0, 1)
    pack(0)
    for c in range(COLS):
        a_wait(2, 0, c)
        a_start(2, 1, c)
    begin(e_copies)
    arrived(y_copy(1), "ywait1")
    a_start(1, 1, 1)
    a_start(3, 1, 1)
    a_wait(3, 0, 0)
    pack(1)
    for c in range(COLS):
        a_wait(3, 1, c)
    pack(2)
    for c in range(COLS):
        a_wait(1, 1, c)
        a_wait(2, 1, c)
    pack(3)
    up(0)
    mix(3)
    mix(2)
    up(1)
    mix(1)
    mix(0)
    up(2)
    for q in range(GROUPS):
        down(2, q)
    up(3)
    for k in (3, 1, 0):
        for q in range(GROUPS):
            down(k, q)
    for q in range(GROUPS):
        third(q)
    for q in range(GROUPS):
        second(q)
    arrived(e_copies, "ewait")
    backward(1)
    for q in (1, 0):
        first(q)
    in_weight_grads()
    down_weight_grad()
    for q in range(GROUPS):
        home(q)
    zeroth(1)
    first_late()
    zeroth(0)
    finish(1)
    finish(0)

    for copy in e_copies:
        copy.wait_send()
    for c in range(COLS):
        for copy in y_copy(c):
            copy.wait_send()
        for slot in range(1, SIDE):
            for dy in range(2):
                for copy in a_copy(slot, dy, c):
                    copy.wait_send()
    for d in range(SIDE):
        for t in range(1, TARGETS):
            b_copy(d, t).wait_send()
    for q in range(GROUPS):
        for k in range(SIDE):
            for t in range(1, TARGETS):
                rb_copy(k, t, q).wait_send()
            ra_copy(k, q).wait_send()
        for k in (1, 3):
            rp_copy(k, q).wait_send()
        ry_copy(q).wait_send()
        mixed_copy(q).wait()


def shards(tokens, routes, gate_weights, w_gate, w_up, w_down, saved_inputs, saved_cotangent):
    rows, width = tokens.shape
    hidden = w_gate.shape[2]
    back_rows = saved_inputs.shape[1]
    anywhere = pl.BlockSpec(memory_space=pl.ANY)
    whole = pl.BlockSpec(memory_space=pltpu.VMEM)
    dma = pltpu.SemaphoreType.DMA
    vm = pltpu.VMEM
    return pl.pallas_call(
        kernel,
        out_shape=(
            jax.ShapeDtypeStruct((rows, width), BF),
            jax.ShapeDtypeStruct((1, width // 2, hidden), F32),
            jax.ShapeDtypeStruct((1, width // 2, hidden), F32),
            jax.ShapeDtypeStruct((1, hidden // 2, width), F32),
        ),
        in_specs=[whole, whole] + [anywhere] * 6,
        out_specs=(anywhere,) * 4,
        scratch_shapes=[
            vm((width, hidden), BF), vm((width, hidden), BF), vm((hidden, width), BF),
            vm((SIDE, 2 * rows, width), BF),
            vm((SIDE, 2, 128, rows), BF), vm((2, 128, rows), F32),
            vm((CHUNK, 2 * rows), F32), vm((CHUNK, 2 * rows), BF), vm((SIDE, 2 * rows, CHUNK), BF),
            vm((SIDE, CHUNK, width), BF), vm((SIDE, CHUNK, width), BF), vm((SIDE, CHUNK, width), BF),
            vm((SIDE, 2 * rows, width), BF), vm((SIDE, rows, width), BF), vm((2, rows, width), BF),
            vm((rows, width), BF), vm((rows, width), BF), vm((rows, width), F32), vm((rows, width), BF),
            vm((2, back_rows, width), BF), vm((2, back_rows, width), BF),
            vm((2, back_rows, hidden), BF), vm((2, back_rows, hidden), BF), vm((2, back_rows, hidden), BF),
            vm((SIDE, CHUNK, hidden), BF),
            vm((2, 2, TILE, hidden), F32), vm((2, hidden // 2, 512), F32),
            dma((6,)), dma((COLS + 1,)), dma((COLS + 1,)), dma((6, COLS + 1)), dma((6, COLS + 1)),
            dma((SIDE, TARGETS)), dma((SIDE, TARGETS)),
            dma((SIDE * GROUPS, TARGETS)), dma((SIDE * GROUPS, TARGETS)),
            dma((2, GROUPS)), dma((2, GROUPS)), dma((SIDE, GROUPS)), dma((SIDE, GROUPS)),
            dma((GROUPS,)), dma((GROUPS,)), dma((2,)), dma((2,)), dma((3, 2)), dma((GROUPS,)),
        ],
        compiler_params=pltpu.CompilerParams(
            collective_id=0, has_side_effects=True, vmem_limit_bytes=62 * 1024 * 1024
        ),
        cost_estimate=pl.CostEstimate(flops=22 * 10**9, bytes_accessed=40 * 10**6, transcendentals=2 * 10**6),
    )(routes.T, gate_weights.T, tokens, w_gate, w_up, w_down, saved_inputs, saved_cotangent)


def solution(mesh):
    return jax.shard_map(
        shards,
        mesh=mesh,
        in_specs=(
            P(("edp", "ep"), None),
            P(("edp", "ep"), None),
            P(("edp", "ep"), None),
            P("ep", None, None),
            P("ep", None, None),
            P("ep", None, None),
            P("ep", "edp", None),
            P("ep", "edp", None),
        ),
        out_specs=(
            P(("edp", "ep"), None),
            P("ep", "edp", None),
            P("ep", "edp", None),
            P("ep", "edp", None),
        ),
        check_vma=False,
    )
```

time: 150 us -> 127 us (0.85)
  Pallas kernels: 139 us -> 115 us
    pallas_call x1, Pallas kernels: 139 us -> 115 us  [shards(): pl.pallas_call(kernel, out_shape=(jax.ShapeDtypeStruct((rows, width), BF)...]
where the time goes in v1:
time: 127 us; the launch traced here: 126 us
  Pallas kernels  115 us (91%)
  local copies, waits for them, and re-layouts  10.5 us (8%)
    pallas_call x1, Pallas kernels, shards(): pl.pallas_call(kernel, out_shape=(jax.ShapeDtypeStruct((rows, width), BF)...  115 us
    unnamed x8, local copies, waits for them, and re-layouts  10.5 us

profile of v1, /device:TPU:1, one launch (start us, length us, event | category | flops | bytes accessed | tf_op | source)
XLA Modules:
  0.0 125.7 jit_solution(13426132156901428239)
XLA Ops:
  0.6 114.6 %shard_map.111 = (bf16[128,2048]{1,0:T(8,128)(2,1)}, f32[1,1024,768]{2,1,0:T(8,128)}, f32[1,1024,768]{2,1,0:T(8,128)}, f32[1,384,2048]{2,1,0:T(8,128)}) custom-call(s32[8,128]{1,0:T(8,128)} %bitcast.2, f32[8,128]{1,0:T(8,128)} %bitcast.3, bf16[128,2048]{1,0:T(8,128)(2,1)} %tokens.1, bf16[1,2048,768]{2,1,0:T(8,128)(2,1)} %w_gate.1, ...), custom_call_target="tpu_custom_call" | custom-call | flops 22000001024 | bytes 40000000 | tf_op jit(solution)/shard_map/pallas_call | solution.py:533
  115.2 1.9 %copy.16 = bf16[128,2048]{1,0:T(8,128)(2,1)} copy(bf16[128,2048]{1,0:T(8,128)(2,1)} %get-tuple-element.8) | data formatting | bytes 1048576
  117.1 0.0 copy-start.1
  117.1 3.9 %copy.17 = f32[1,1024,768]{2,1,0:T(8,128)} copy(f32[1,1024,768]{2,1,0:T(8,128)} %get-tuple-element.9) | data formatting | bytes 6291456
  121.0 0.0 copy-done.1
  121.0 0.0 copy-start
  121.0 1.7 %copy.18 = f32[1,1024,768]{2,1,0:T(8,128)} copy(f32[1,1024,768]{2,1,0:T(8,128)S(1)} %copy-done.1) | data formatting | bytes 6291456
  122.7 1.4 %copy-done = f32[1,384,2048]{2,1,0:T(8,128)S(1)} copy-done((f32[1,384,2048]{2,1,0:T(8,128)S(1)}, f32[1,384,2048]{2,1,0:T(8,128)}, u32[]{:S(2)}) %copy-start) | copy-done | bytes 3145752
  124.1 1.7 %copy.19 = f32[1,384,2048]{2,1,0:T(8,128)} copy(f32[1,384,2048]{2,1,0:T(8,128)S(1)} %copy-done) | data formatting | bytes 6291456
Async XLA Ops:
  117.1 3.9 %copy-start.1 = (f32[1,1024,768]{2,1,0:T(8,128)S(1)}, f32[1,1024,768]{2,1,0:T(8,128)}, u32[]{:S(2)}) copy-start(f32[1,1024,768]{2,1,0:T(8,128)} %get-tuple-element.10) | copy-start | bytes 9437188
  121.0 3.0 %copy-start = (f32[1,384,2048]{2,1,0:T(8,128)S(1)}, f32[1,384,2048]{2,1,0:T(8,128)}, u32[]{:S(2)}) copy-start(f32[1,384,2048]{2,1,0:T(8,128)} %get-tuple-element.11) | copy-start | bytes 9437188

commit v2 on v1

--- a/solution.py
+++ b/solution.py
@@ -39,8 +39,8 @@
     routes, gates, tokens, w_gate, w_up, w_down, saved_x, saved_y,
     mixed, grad_gate, grad_up, grad_down,
     wg, wu, wd, blocks, aux, aux32, hot, hot_lhs, mix_lhs, packed, recv, back, part, gathered, passed,
-    y_send, y_recv, total, result, xs, ys, hid, dgs, dus, hbuf, stage_a, stage_b,
-    load_sem, y_s, y_r, a_s, a_r, b_s, b_r, rb_s, rb_r, rp_s, rp_r, ra_s, ra_r, ry_s, ry_r, e_s, e_r, out_sem, mix_sem,
+    y_send, y_recv, total, xs, ys, hid, dgs, dus, hbuf,
+    load_sem, y_s, y_r, a_s, a_r, b_s, b_r, rb_s, rb_r, rp_s, rp_r, ra_s, ra_r, ry_s, ry_r, e_s, e_r,
 ):
     width = blocks.shape[-1]
     rows = blocks.shape[1] // 2
@@ -368,70 +368,39 @@
             each_tile(q, body)
             ry_copy(q).start()
 
-    def mixed_copy(q):
-        return pltpu.make_async_copy(result.at[:, group(q)], mixed.at[:, group(q)], mix_sem.at[q])
-
     def finish(q):
         arrived([ry_copy(q), ra_copy(1, q), ra_copy(0, q)], f"lastwait{q}")
 
         def body(cols):
             value = total[:, cols] + y_recv[:, cols].astype(F32)
             value = value + gathered[0, :, cols].astype(F32) + gathered[1, :, cols].astype(F32)
-            result[:, cols] = value.astype(BF)
+            mixed[:, cols] = value.astype(BF)
 
         each_tile(q, body)
-        mixed_copy(q).start()
-
-    def out_copies(kind, n):
-        slot = lax.rem(n, 2)
-        if kind == 2:
-            return pltpu.make_async_copy(stage_b.at[slot], grad_down.at[0, :, tile(n, stage_b.shape[2])],
-                                         out_sem.at[2, slot])
-        ref = grad_gate if kind == 0 else grad_up
-        return pltpu.make_async_copy(stage_a.at[kind, slot], ref.at[0, tile(n)], out_sem.at[kind, slot])
 
     def in_weight_grads():
         def body(n):
-            @pl.when(n >= 2)
-            def _():
-                for kind in range(2):
-                    out_copies(kind, n - 2).wait()
-
             cols = pl.ds(pl.multiple_of(replica * half_width + n * TILE, TILE), TILE)
-            slot = lax.rem(n, 2)
-            for kind, source in ((0, dgs), (1, dus)):
+            for out, source in ((grad_gate, dgs), (grad_up, dus)):
                 sums = [dot(xs[r, :, cols], source[r], ((0,), (0,))).astype(BF).astype(F32) for r in range(2)]
-                stage_a[kind, slot] = sums[0] + sums[1]
-                out_copies(kind, n).start()
-
-        count = half_width // TILE
+                out[0, tile(n), :] = sums[0] + sums[1]
+
         with jax.named_scope("gradin"):
-            loop(count, body)
-            for n in (count - 2, count - 1):
-                for kind in range(2):
-                    out_copies(kind, n).wait()
+            loop(half_width // TILE, body)
 
     def down_weight_grad():
-        size = stage_b.shape[2]
+        size = 512
 
         def body(n):
-            @pl.when(n >= 2)
-            def _():
-                out_copies(2, n - 2).wait()
-
             own_cols = pl.ds(pl.multiple_of(replica * half_hidden, 128), half_hidden)
-            slot = lax.rem(n, 2)
             sums = [
                 dot(hid[r, :, own_cols], ys[r, :, tile(n, size)], ((0,), (0,))).astype(BF).astype(F32)
                 for r in range(2)
             ]
-            stage_b[slot] = sums[0] + sums[1]
-            out_copies(2, n).start()
+            grad_down[0, :, tile(n, size)] = sums[0] + sums[1]
 
         with jax.named_scope("graddown"):
             loop(width // size, body)
-            for n in (width // size - 2, width // size - 1):
-                out_copies(2, n).wait()
 
     begin(y_copy(0))
     a_start(1, 0, 0)
@@ -519,7 +488,19 @@
         for k in (1, 3):
             rp_copy(k, q).wait_send()
         ry_copy(q).wait_send()
-        mixed_copy(q).wait()
+
+
+def flush(*refs):
+    count = len(refs) // 2
+    sems = refs[-1]
+    copies = [
+        pltpu.make_async_copy(source, target, sems.at[n])
+        for n, (source, target) in enumerate(zip(refs[:count], refs[count : 2 * count]))
+    ]
+    for copy in copies:
+        copy.start()
+    for copy in copies:
+        copy.wait()
 
 
 def shards(tokens, routes, gate_weights, w_gate, w_up, w_down, saved_inputs, saved_cotangent):
@@ -530,16 +511,16 @@
     whole = pl.BlockSpec(memory_space=pltpu.VMEM)
     dma = pltpu.SemaphoreType.DMA
     vm = pltpu.VMEM
-    return pl.pallas_call(
+    held = pl.pallas_call(
         kernel,
         out_shape=(
-            jax.ShapeDtypeStruct((rows, width), BF),
-            jax.ShapeDtypeStruct((1, width // 2, hidden), F32),
-            jax.ShapeDtypeStruct((1, width // 2, hidden), F32),
-            jax.ShapeDtypeStruct((1, hidden // 2, width), F32),
+            pltpu.VMEM((rows, width), BF),
+            pltpu.VMEM((1, width // 2, hidden), F32),
+            pltpu.VMEM((1, width // 2, hidden), F32),
+            pltpu.VMEM((1, hidden // 2, width), F32),
         ),
         in_specs=[whole, whole] + [anywhere] * 6,
-        out_specs=(anywhere,) * 4,
+        out_specs=(whole,) * 4,
         scratch_shapes=[
             vm((width, hidden), BF), vm((width, hidden), BF), vm((hidden, width), BF),
             vm((SIDE, 2 * rows, width), BF),
@@ -547,22 +528,30 @@
             vm((CHUNK, 2 * rows), F32), vm((CHUNK, 2 * rows), BF), vm((SIDE, 2 * rows, CHUNK), BF),
             vm((SIDE, CHUNK, width), BF), vm((SIDE, CHUNK, width), BF), vm((SIDE, CHUNK, width), BF),
             vm((SIDE, 2 * rows, width), BF), vm((SIDE, rows, width), BF), vm((2, rows, width), BF),
-            vm((rows, width), BF), vm((rows, width), BF), vm((rows, width), F32), vm((rows, width), BF),
+            vm((rows, width), BF), vm((rows, width), BF), vm((rows, width), F32),
             vm((2, back_rows, width), BF), vm((2, back_rows, width), BF),
             vm((2, back_rows, hidden), BF), vm((2, back_rows, hidden), BF), vm((2, back_rows, hidden), BF),
             vm((SIDE, CHUNK, hidden), BF),
-            vm((2, 2, TILE, hidden), F32), vm((2, hidden // 2, 512), F32),
             dma((6,)), dma((COLS + 1,)), dma((COLS + 1,)), dma((6, COLS + 1)), dma((6, COLS + 1)),
             dma((SIDE, TARGETS)), dma((SIDE, TARGETS)),
             dma((SIDE * GROUPS, TARGETS)), dma((SIDE * GROUPS, TARGETS)),
             dma((2, GROUPS)), dma((2, GROUPS)), dma((SIDE, GROUPS)), dma((SIDE, GROUPS)),
-            dma((GROUPS,)), dma((GROUPS,)), dma((2,)), dma((2,)), dma((3, 2)), dma((GROUPS,)),
+            dma((GROUPS,)), dma((GROUPS,)), dma((2,)), dma((2,)),
         ],
         compiler_params=pltpu.CompilerParams(
-            collective_id=0, has_side_effects=True, vmem_limit_bytes=62 * 1024 * 1024
+            collective_id=0, has_side_effects=True, vmem_limit_bytes=53 * 1024 * 1024
         ),
         cost_estimate=pl.CostEstimate(flops=22 * 10**9, bytes_accessed=40 * 10**6, transcendentals=2 * 10**6),
     )(routes.T, gate_weights.T, tokens, w_gate, w_up, w_down, saved_inputs, saved_cotangent)
+    return pl.pallas_call(
+        flush,
+        out_shape=tuple(jax.ShapeDtypeStruct(h.shape, h.dtype) for h in held),
+        in_specs=[anywhere] * 4,
+        out_specs=(anywhere,) * 4,
+        scratch_shapes=[dma((4,))],
+        compiler_params=pltpu.CompilerParams(vmem_limit_bytes=1024 * 1024),
+        cost_estimate=pl.CostEstimate(flops=0, bytes_accessed=20 * 10**6, transcendentals=0),
+    )(*[pltpu.with_memory_space_constraint(h, pltpu.VMEM) for h in held])
 
 
 def solution(mesh):

time: 127 us -> 118 us (0.929)
  local copies, waits for them, and re-layouts: 10.5 us -> 0 us
  Pallas kernels: 115 us -> 117 us
    unnamed x8 -> x0, local copies, waits for them, and re-layouts: 10.5 us -> none
    pallas_call x1 -> x2, Pallas kernels: 115 us -> 117 us  [the longest x1 113 us: shards(): pl.pallas_call(kernel, out_shape=(pltpu.VMEM((rows, width), BF), pltpu.VM...]
where the time goes in v2:
time: 118 us
  Pallas kernels  117 us (99%)
    pallas_call x1, Pallas kernels, shards(): pl.pallas_call(kernel, out_shape=(pltpu.VMEM((rows, width), BF), pltpu.VM...  113 us
    pallas_call x1, Pallas kernels, shards(): pl.pallas_call(flush, out_shape=tuple((jax.ShapeDtypeStruct(h.shape, h.dt...  3.94 us

profile of v2, /device:TPU:1, one launch (start us, length us, event | category | flops | bytes accessed | tf_op | source)
XLA Modules:
  0.0 117.9 jit_solution(10201823915503267747)
XLA Ops:
  0.6 113.3 %shard_map.111 = (bf16[128,2048]{1,0:T(8,128)(2,1)S(1)}, f32[1,1024,768]{2,1,0:T(8,128)S(1)}, f32[1,1024,768]{2,1,0:T(8,128)S(1)}, f32[1,384,2048]{2,1,0:T(8,128)S(1)}) custom-call(s32[8,128]{1,0:T(8,128)} %bitcast.2, f32[8,128]{1,0:T(8,128)} %bitcast.3, bf16[128,2048]{1,0:T(8,128)(2,1)} %tokens.1, bf16[1,2048,768]{2,1,0:T(8,128)(2,1)} %w_gate.1, ...), custom_call_target="tpu_custom_call" | custom-call | flops 22000001024 | bytes 40000000 | tf_op jit(solution)/shard_map/pallas_call | solution.py:514
  114.0 3.9 %shard_map.112 = (bf16[128,2048]{1,0:T(8,128)(2,1)}, f32[1,1024,768]{2,1,0:T(8,128)}, f32[1,1024,768]{2,1,0:T(8,128)}, f32[1,384,2048]{2,1,0:T(8,128)}) custom-call(bf16[128,2048]{1,0:T(8,128)(2,1)S(1)} %get-tuple-element.8.refs_0_, f32[1,1024,768]{2,1,0:T(8,128)S(1)} %get-tuple-element.9.refs_1_, f32[1,1024,768]{2,1,0:T(8,128)S(1)} %get-tuple-element.10.refs_2_, ...), custom_call_target="tpu_custom_call" | custom-call | bytes 20000000 | tf_op jit(solution)/shard_map/pallas_call | solution.py:546

commit v3 on v2

--- a/solution.py
+++ b/solution.py
@@ -207,15 +207,24 @@
 
     def b_copy(d, t):
         span = pl.ds(PAIR * t, PAIR)
-        return remote(packed.at[d, span], recv.at[d, span], b_s.at[d, t], b_r.at[d, t], at(forward_to(t)))
+        return remote(packed.at[d, span], recv.at[d, span], b_s.at[d], b_r.at[d], at(forward_to(t)))
+
+    others = pl.ds(PAIR, CHUNK - PAIR)
+
+    def b_all(d):
+        return remote(packed.at[d, others], recv.at[d, others], b_s.at[d], b_r.at[d], y_peer)
 
     def group(q):
         return pl.ds(q * per_group * TILE, per_group * TILE)
 
     def rb_copy(d, t, q):
         span = pl.ds(PAIR * t, PAIR)
-        return remote(recv.at[d, span, group(q)], back.at[d, span, group(q)], rb_s.at[q * SIDE + d, t],
-                      rb_r.at[q * SIDE + d, t], at(forwarder(t)))
+        return remote(recv.at[d, span, group(q)], back.at[d, span, group(q)], rb_s.at[q, d],
+                      rb_r.at[q, d], at(forwarder(t)))
+
+    def rb_all(d, q):
+        return remote(recv.at[d, others, group(q)], back.at[d, others, group(q)], rb_s.at[q, d],
+                      rb_r.at[q, d], y_peer)
 
     def pack(d):
         with jax.named_scope(f"pack{d}"):
@@ -229,13 +238,12 @@
                 recv[d, 0:PAIR, cols] = rows_out[0:PAIR]
 
             loop(tiles, body)
-            for t in (4, 5, 2, 3, 6, 7, 1):
+            for t in (2, 6, 3, 7, 4, 5, 1):
                 b_copy(d, t).start()
 
     def up(d):
         with jax.named_scope(f"upwait{d}"):
-            for t in range(1, TARGETS):
-                b_copy(d, t).wait_recv()
+            b_all(d).wait_recv()
 
         def body(n):
             cols = tile(n)
@@ -255,7 +263,7 @@
 
         with jax.named_scope(f"down{d}{q}"):
             loop(per_group, body)
-            for t in (4, 5, 2, 3, 6, 7, 1):
+            for t in (2, 3, 6, 7, 4, 5, 1):
                 rb_copy(d, t, q).start()
 
     def mix(d):
@@ -273,8 +281,11 @@
     def ra_wait(k, q):
         ra_copy(k, q).wait_recv()
 
+    def low(q):
+        return q < GROUPS // 2
+
     def rp_copy(k, q):
-        peer = y_peer if k == 3 else (behind if q == 0 else ahead)
+        peer = y_peer if k == 3 else (behind if low(q) else ahead)
         return remote(part.at[k, half(1), group(q)], passed.at[k // 2, :, group(q)],
                       rp_s.at[k // 2, q], rp_r.at[k // 2, q], peer)
 
@@ -283,8 +294,7 @@
 
     def returned(k, q):
         with jax.named_scope(f"rbwait{k}{q}"):
-            for t in range(1, TARGETS):
-                rb_copy(k, t, q).wait_recv()
+            rb_all(k, q).wait_recv()
 
     def each_tile(q, body):
         loop(per_group, lambda n: body(tile(n + q * per_group)))
@@ -319,36 +329,35 @@
         def body(cols):
             value = dot(mix_lhs[1], back[1, :, cols])
             part[1, half(1), cols] = (value[rows : 2 * rows] + passed[1, :, cols].astype(F32)).astype(BF)
-            if q == 0:
+            if low(q):
                 part[1, half(0), cols] = value[0:rows].astype(BF)
 
         with jax.named_scope(f"first{q}"):
             each_tile(q, body)
             rp_copy(1, q).start()
-            if q == 0:
+            if low(q):
                 ra_copy(1, q).start()
 
-    def first_late():
-        q = 1
+    def first_late(q):
         arrived([rp_copy(1, q)], f"rpwait1{q}")
 
         def body(cols):
             value = dot(mix_lhs[1, half(0), :], back[1, :, cols])
             part[1, half(0), cols] = (value + passed[0, :, cols].astype(F32)).astype(BF)
 
-        with jax.named_scope("firstlate"):
+        with jax.named_scope(f"firstlate{q}"):
             each_tile(q, body)
             ra_copy(1, q).start()
 
     def zeroth(q):
         returned(0, q)
-        if q == 0:
+        if low(q):
             arrived([rp_copy(1, q)], f"rpwait1{q}")
 
         def body(cols):
             value = dot(mix_lhs[0], back[0, :, cols])
             rest = value[rows : 2 * rows]
-            if q == 0:
+            if low(q):
                 rest = rest + passed[0, :, cols].astype(F32)
             part[0, half(1), cols] = rest.astype(BF)
             total[:, cols] = value[0:rows]
@@ -446,6 +455,7 @@
     up(2)
     for q in range(GROUPS):
         down(2, q)
+    low_groups, high_groups = tuple(range(GROUPS // 2)), tuple(range(GROUPS // 2, GROUPS))
     up(3)
     for k in (3, 1, 0):
         for q in range(GROUPS):
@@ -454,40 +464,46 @@
         third(q)
     for q in range(GROUPS):
         second(q)
+    for pair in zip(high_groups, low_groups):
+        for q in pair:
+            first(q)
     arrived(e_copies, "ewait")
     backward(1)
-    for q in (1, 0):
-        first(q)
     in_weight_grads()
-    down_weight_grad()
     for q in range(GROUPS):
         home(q)
-    zeroth(1)
-    first_late()
-    zeroth(0)
-    finish(1)
-    finish(0)
-
-    for copy in e_copies:
-        copy.wait_send()
-    for c in range(COLS):
-        for copy in y_copy(c):
+    for q, p in zip(high_groups, low_groups):
+        zeroth(q)
+        first_late(q)
+        zeroth(p)
+    down_weight_grad()
+    with jax.named_scope("drain"):
+        for copy in e_copies:
             copy.wait_send()
-        for slot in range(1, SIDE):
-            for dy in range(2):
-                for copy in a_copy(slot, dy, c):
-                    copy.wait_send()
-    for d in range(SIDE):
-        for t in range(1, TARGETS):
-            b_copy(d, t).wait_send()
-    for q in range(GROUPS):
-        for k in range(SIDE):
-            for t in range(1, TARGETS):
-                rb_copy(k, t, q).wait_send()
-            ra_copy(k, q).wait_send()
-        for k in (1, 3):
-            rp_copy(k, q).wait_send()
-        ry_copy(q).wait_send()
+        for c in range(COLS):
+            for copy in y_copy(c):
+                copy.wait_send()
+            for slot in range(1, SIDE):
+                for dy in range(2):
+                    for copy in a_copy(slot, dy, c):
+                        copy.wait_send()
+        for d in range(SIDE):
+            b_all(d).wait_send()
+        for q in range(GROUPS):
+            for k in range(SIDE):
+                rb_all(k, q).wait_send()
+            for k in (1, 3):
+                rp_copy(k, q).wait_send()
+            for k in (2, 3):
+                ra_copy(k, q).wait_send()
+    for q, p in zip(high_groups, low_groups):
+        finish(q)
+        finish(p)
+    with jax.named_scope("lastdrain"):
+        for q in range(GROUPS):
+            for k in (0, 1):
+                ra_copy(k, q).wait_send()
+            ry_copy(q).wait_send()
 
 
 def flush(*refs):
@@ -533,8 +549,8 @@
             vm((2, back_rows, hidden), BF), vm((2, back_rows, hidden), BF), vm((2, back_rows, hidden), BF),
             vm((SIDE, CHUNK, hidden), BF),
             dma((6,)), dma((COLS + 1,)), dma((COLS + 1,)), dma((6, COLS + 1)), dma((6, COLS + 1)),
-            dma((SIDE, TARGETS)), dma((SIDE, TARGETS)),
-            dma((SIDE * GROUPS, TARGETS)), dma((SIDE * GROUPS, TARGETS)),
+            dma((SIDE,)), dma((SIDE,)),
+            dma((GROUPS, SIDE)), dma((GROUPS, SIDE)),
             dma((2, GROUPS)), dma((2, GROUPS)), dma((SIDE, GROUPS)), dma((SIDE, GROUPS)),
             dma((GROUPS,)), dma((GROUPS,)), dma((2,)), dma((2,)),
         ],

time: 118 us -> 114 us (0.966)
  Pallas kernels: 117 us -> 113 us
    pallas_call x1, Pallas kernels: 113 us -> 109 us  [shards(): pl.pallas_call(kernel, out_shape=(pltpu.VMEM((rows, width), BF), pltpu.VM...]
where the time goes in v3:
time: 114 us
  Pallas kernels  113 us (99%)
    pallas_call x1, Pallas kernels, shards(): pl.pallas_call(kernel, out_shape=(pltpu.VMEM((rows, width), BF), pltpu.VM...  109 us
    pallas_call x1, Pallas kernels, shards(): pl.pallas_call(flush, out_shape=tuple((jax.ShapeDtypeStruct(h.shape, h.dt...  3.94 us

profile of v3, /device:TPU:1, one launch (start us, length us, event | category | flops | bytes accessed | tf_op | source)
XLA Modules:
  0.0 114.1 jit_solution(986558091277142508)
XLA Ops:
  0.6 109.5 %shard_map.111 = (bf16[128,2048]{1,0:T(8,128)(2,1)S(1)}, f32[1,1024,768]{2,1,0:T(8,128)S(1)}, f32[1,1024,768]{2,1,0:T(8,128)S(1)}, f32[1,384,2048]{2,1,0:T(8,128)S(1)}) custom-call(s32[8,128]{1,0:T(8,128)} %bitcast.2, f32[8,128]{1,0:T(8,128)} %bitcast.3, bf16[128,2048]{1,0:T(8,128)(2,1)} %tokens.1, bf16[1,2048,768]{2,1,0:T(8,128)(2,1)} %w_gate.1, ...), custom_call_target="tpu_custom_call" | custom-call | flops 22000001024 | bytes 40000000 | tf_op jit(solution)/shard_map/pallas_call | solution.py:530
  110.1 3.9 %shard_map.112 = (bf16[128,2048]{1,0:T(8,128)(2,1)}, f32[1,1024,768]{2,1,0:T(8,128)}, f32[1,1024,768]{2,1,0:T(8,128)}, f32[1,384,2048]{2,1,0:T(8,128)}) custom-call(bf16[128,2048]{1,0:T(8,128)(2,1)S(1)} %get-tuple-element.8.refs_0_, f32[1,1024,768]{2,1,0:T(8,128)S(1)} %get-tuple-element.9.refs_1_, f32[1,1024,768]{2,1,0:T(8,128)S(1)} %get-tuple-element.10.refs_2_, ...), custom_call_target="tpu_custom_call" | custom-call | bytes 20000000 | tf_op jit(solution)/shard_map/pallas_call | solution.py:562

commit v4 on v3

--- a/solution.py
+++ b/solution.py
@@ -433,12 +433,12 @@
     for c in range(COLS):
         a_wait(2, 0, c)
         a_start(2, 1, c)
-    begin(e_copies)
     arrived(y_copy(1), "ywait1")
     a_start(1, 1, 1)
     a_start(3, 1, 1)
     a_wait(3, 0, 0)
     pack(1)
+    begin(e_copies)
     for c in range(COLS):
         a_wait(3, 1, c)
     pack(2)

time: 114 us -> 114 us (level)
  no operation moved by 1% of the time
where the time goes in v4:
time: 114 us
  Pallas kernels  113 us (99%)
    pallas_call x1, Pallas kernels, shards(): pl.pallas_call(kernel, out_shape=(pltpu.VMEM((rows, width), BF), pltpu.VM...  109 us
    pallas_call x1, Pallas kernels, shards(): pl.pallas_call(flush, out_shape=tuple((jax.ShapeDtypeStruct(h.shape, h.dt...  3.94 us

profile of v4, /device:TPU:1, one launch (start us, length us, event | category | flops | bytes accessed | tf_op | source)
XLA Modules:
  0.0 114.1 jit_solution(4897612962970712686)
XLA Ops:
  0.6 109.5 %shard_map.111 = (bf16[128,2048]{1,0:T(8,128)(2,1)S(1)}, f32[1,1024,768]{2,1,0:T(8,128)S(1)}, f32[1,1024,768]{2,1,0:T(8,128)S(1)}, f32[1,384,2048]{2,1,0:T(8,128)S(1)}) custom-call(s32[8,128]{1,0:T(8,128)} %bitcast.2, f32[8,128]{1,0:T(8,128)} %bitcast.3, bf16[128,2048]{1,0:T(8,128)(2,1)} %tokens.1, bf16[1,2048,768]{2,1,0:T(8,128)(2,1)} %w_gate.1, ...), custom_call_target="tpu_custom_call" | custom-call | flops 22000001024 | bytes 40000000 | tf_op jit(solution)/shard_map/pallas_call | solution.py:530
  110.1 3.9 %shard_map.112 = (bf16[128,2048]{1,0:T(8,128)(2,1)}, f32[1,1024,768]{2,1,0:T(8,128)}, f32[1,1024,768]{2,1,0:T(8,128)}, f32[1,384,2048]{2,1,0:T(8,128)}) custom-call(bf16[128,2048]{1,0:T(8,128)(2,1)S(1)} %get-tuple-element.8.refs_0_, f32[1,1024,768]{2,1,0:T(8,128)S(1)} %get-tuple-element.9.refs_1_, f32[1,1024,768]{2,1,0:T(8,128)S(1)} %get-tuple-element.10.refs_2_, ...), custom_call_target="tpu_custom_call" | custom-call | bytes 20000000 | tf_op jit(solution)/shard_map/pallas_call | solution.py:562
